TPU v7x, 32 devices: a whole 2x2x4 slice. The times are simulated.
32 devices in a mesh: section: 2 (over x), tensor: 4 (over z), dp: 4 (over y, core).
Axes of the slice: x: 2, y: 2, z: 4, core: 2. Of those that a mesh axis runs over, the one named last changes fastest.
Arguments:
- tokens: bfloat16 [16, 4096], P(None, ('section', 'dp')), may hold values from -100 to 100
- attn_gain: float32 [4096], P(('section', 'dp')), may hold values from 0.1 to 1.9
- qkv_weight: bfloat16 [4096, 10240], P(('section', 'dp'), 'tensor'), may hold values from -0.09375 to 0.09375
- qkv_order: int32 [10], replicated, may hold values from 0 to 9, each once
- cache_keys: bfloat16 [16, 8, 4096, 128], P(('section', 'dp'), 'tensor'), may hold values from -1300 to 1300
- cache_values: bfloat16 [16, 8, 4096, 128], P(('section', 'dp'), 'tensor'), may hold values from -6 to 6
- cache_len: int32 [16], P(('section', 'dp')), may hold values from 2 to 4096, as said below
- out_weight: bfloat16 [8192, 4096], P('tensor', ('section', 'dp')), may hold values from -0.0625 to 0.0625
- ffn_gain: float32 [4096], P(('section', 'dp')), may hold values from 0.1 to 1.9
- gate_up: bfloat16 [2, 4096, 28672], P(None, ('section', 'dp'), 'tensor'), may hold values from -0.09375 to 0.09375
- down_weight: bfloat16 [28672, 4096], P('tensor', ('section', 'dp')), may hold values from -0.03125 to 0.03125
Outputs:
- layer_out: bfloat16 [16, 4096], P(None, ('section', 'dp'))
Inputs may be any that keep to these rules, and one draw needn't show every extreme that they name: qkv_order is a permutation of 0 to 9, the same for every key-value group. `cache_len`: at least one sequence has all 4096 positions valid.
All inputs are finite; a program needn't handle non-finite values.
Results may differ from a plain program's by a relative error of at most 0.0065.
Values may be sent and summed in bfloat16 or wider, within the bound.
A program may use at most 64 MiB of HBM per device.

v0:
```python
import jax
import jax.numpy as jnp
from jax import lax
from jax.sharding import PartitionSpec as P

D = 4096
HEADS = 64
KV_HEADS = 8
HD = 128
LEN = 4096
GROUP = 10


def normalize(stream, gain_vec):
    wide = stream.astype(jnp.float32)
    squares = lax.psum(jnp.sum(wide * wide, axis=1), ("section", "dp"))
    factor = lax.rsqrt(squares / D + 1e-05)
    return (wide * factor[:, None] * gain_vec[None, :]).astype(jnp.bfloat16)


def rotate(vector, cosine, sine_part):
    half_dim = vector.shape[-1] // 2
    first_half = vector[..., :half_dim]
    second = vector[..., half_dim:]
    return jnp.concatenate(
        [first_half * cosine - second * sine_part, second * cosine + first_half * sine_part],
        axis=-1,
    )


def project_rows(row_block, weight_cols):
    return jnp.dot(
        lax.all_gather(row_block, ("section", "dp"), axis=0, tiled=True),
        weight_cols,
        preferred_element_type=jnp.float32,
    )


def add_residual(base_rows, partial_sum):
    summed = lax.psum(partial_sum, "tensor")
    return (base_rows.astype(jnp.float32) + summed).astype(jnp.bfloat16)


def body(
    tokens,
    attn_gain,
    qkv_weight,
    qkv_order,
    cache_keys,
    cache_values,
    cache_len,
    out_weight,
    ffn_gain,
    gate_up,
    down_weight,
):
    seq_count = cache_len.shape[0]
    local_groups = cache_keys.shape[1]
    per_group = HEADS // KV_HEADS
    normed = normalize(tokens, attn_gain)
    row_block = normed
    joined_cols = lax.psum_scatter(
        jnp.dot(row_block, qkv_weight, preferred_element_type=jnp.float32),
        ("section", "dp"),
        scatter_dimension=0,
        tiled=True,
    )
    blocks = joined_cols.reshape(seq_count, local_groups, GROUP, HD)
    onehot = (qkv_order[:, None] == jnp.arange(GROUP, dtype=jnp.int32)[None, :]).astype(jnp.float32)
    logical = jnp.einsum("bgjd,ji->bgid", blocks, onehot, precision=lax.Precision.HIGHEST)
    half_dim = HD // 2
    inv_freq = 500000.0 ** (-(2.0 * jnp.arange(half_dim, dtype=jnp.float32)) / HD)
    angles = cache_len.astype(jnp.float32)[:, None] * inv_freq[None, :]
    cosine = jnp.cos(angles)
    sine_part = jnp.sin(angles)
    queries = rotate(
        logical[:, :, :per_group], cosine[:, None, None, :], sine_part[:, None, None, :]
    ).astype(jnp.bfloat16)
    new_key = rotate(logical[:, :, per_group], cosine[:, None, :], sine_part[:, None, :]).astype(
        jnp.bfloat16
    )
    new_value = logical[:, :, per_group + 1].astype(jnp.bfloat16)
    inv_scale = 1.0 / jnp.sqrt(jnp.float32(HD))
    scores = (
        jnp.einsum("bgpd,bgld->bgpl", queries, cache_keys, preferred_element_type=jnp.float32)
        * inv_scale
    )
    own_score = (
        jnp.einsum("bgpd,bgd->bgp", queries, new_key, preferred_element_type=jnp.float32)
        * inv_scale
    )
    valid_mask = jnp.arange(LEN, dtype=jnp.int32)[None, :] < cache_len[:, None]
    masked = jnp.where(valid_mask[:, None, None, :], scores, -jnp.inf)
    peak = jnp.maximum(jnp.max(masked, axis=-1), own_score)
    weights = jnp.exp(masked - peak[..., None])
    own_weight = jnp.exp(own_score - peak)
    denom_sum = jnp.sum(weights, axis=-1) + own_weight
    probabilities = (weights / denom_sum[..., None]).astype(jnp.bfloat16)
    own_prob = (own_weight / denom_sum).astype(jnp.bfloat16)
    mixed_heads = jnp.einsum(
        "bgpl,bgld->bgpd", probabilities, cache_values, preferred_element_type=jnp.float32
    )
    mixed_heads = (
        mixed_heads
        + own_prob.astype(jnp.float32)[..., None] * new_value.astype(jnp.float32)[:, :, None, :]
    )
    attended = mixed_heads.astype(jnp.bfloat16).reshape(seq_count, -1)
    hidden_state = add_residual(tokens, project_rows(attended, out_weight))
    ffn_normed = normalize(hidden_state, ffn_gain)
    row_block = ffn_normed
    gate_and_up = lax.psum_scatter(
        jnp.einsum("rd,kdf->rkf", row_block, gate_up, preferred_element_type=jnp.float32),
        ("section", "dp"),
        scatter_dimension=0,
        tiled=True,
    )
    activated = (jax.nn.silu(gate_and_up[:, 0]) * gate_and_up[:, 1]).astype(jnp.bfloat16)
    return add_residual(hidden_state, project_rows(activated, down_weight))


def solution(mesh):
    return jax.shard_map(
        body,
        mesh=mesh,
        in_specs=(
            P(None, ("section", "dp")),
            P(("section", "dp")),
            P(("section", "dp"), "tensor"),
            P(),
            P(("section", "dp"), "tensor", None, None),
            P(("section", "dp"), "tensor", None, None),
            P(("section", "dp")),
            P("tensor", ("section", "dp")),
            P(("section", "dp")),
            P(None, ("section", "dp"), "tensor"),
            P("tensor", ("section", "dp")),
        ),
        out_specs=P(None, ("section", "dp")),
        check_vma=False,
    )
```

profile of v0, /device:TPU:0, one launch (start us, length us, event | category | flops | bytes accessed | tf_op | source)
XLA Modules:
  0.0 227.4 jit_solution(6629242835967836412)
XLA Ops:
  6.5 0.0 copy-start
  6.5 0.0 all-reduce.5.cloned.1.call-start
  6.5 1.0 fusion.7
  7.5 15.1 %psum.28 = f32[16]{0:T(128)S(1)} all-reduce(f32[16]{0:T(128)S(1)} %fusion.7), channel_id=1, replica_groups=mesh['section'=2,'tensor'=4,'dp'=4] {'section','dp'}, use_global_device_ids=true, to_apply=%region_1.0 | all-reduce | flops 16 | bytes 128 | tf_op jit(solution)/shard_map/psum | solution.py:16
  22.7 0.0 copy-done
  22.7 1.9 fusion.19
  24.6 0.0 all-reduce.5.cloned.1.call-update
  24.6 0.0 all-reduce.7.cloned.1.call-start
  24.6 0.7 convert_element_type.47
  25.3 0.7 iota_compare_fusion
  26.0 0.1 multiply_cosine_fusion
  26.2 1.2 dynamic-slice
  28.1 48.3 %all-reduce.5.cloned.1.call-done = f32[16,2560]{1,0:T(8,128)} async-done(((f32[16,2560]{1,0:T(8,128)}), f32[16,2560]{1,0:T(8,128)}) %all-reduce.5.cloned.1.call-update) | async-done | bytes 163856
  76.4 0.9 constant_dynamic-slice_fusion
  77.3 0.0 copy-start.1
  77.3 0.9 convolution_bitcast_fusion
  78.3 0.1 subtract_convert_fusion
  78.4 0.1 subtract_convert_fusion.1
  78.5 0.1 maximum_bitcast_fusion
  78.5 0.2 fusion.29
  78.7 3.5 %fusion.36 = (f32[2,2,8]{2,1,0:T(2,128)S(1)}, f32[2,2,8,4096]{3,2,1,0:T(8,128)S(1)}) fusion(bf16[2,2,4096,128]{3,2,1,0:T(8,128)(2,1)} %param.15, bf16[2,2,8,64]{3,2,1,0:T(8,128)(2,1)S(1)} %get-tuple-element.8, bf16[2,2,8,64]{3,2,1,0:T(8,128)(2,1)S(1)} %get-tuple-element.7, pred[2,4096]{1,0:T(4,128)(4,1)S(1)} %iota_compare_fusion), kind=kOutput, calls=%fused_computation.64 | convolution fusion | flops 33964000 | bytes 4735104 | tf_op jit(solution)/shard_map/bgpd,bgld->bgpl/dot_general | solution.py:85
  82.2 0.0 copy-start.2
  82.2 0.0 copy-start.3
  82.3 0.2 fusion.2
  82.5 0.0 copy-done.1
  82.5 0.7 fusion.1
  83.3 10.0 %all-gather = bf16[8,2,2048]{2,1,0:T(2,128)(2,1)S(1)} all-gather(bf16[1,2,2048]{2,1,0:T(2,128)(2,1)S(1)} %reshape.129), channel_id=1, replica_groups=mesh['section'=2,'tensor'=4,'dp'=4] {'section','dp'}, dimensions={0}, use_global_device_ids=true | all-gather | bytes 73728 | tf_op jit(solution)/shard_map/all_gather | solution.py:33
  93.3 2.0 fusion.37
  95.3 19.0 %psum.29 = f32[16,512]{1,0:T(8,128)S(1)} all-reduce(f32[16,512]{1,0:T(8,128)S(1)} %fusion.37), channel_id=1, replica_groups=mesh['section'=2,'tensor'=4,'dp'=4] {'tensor'}, use_global_device_ids=true, to_apply=%region_5.6 | all-reduce | flops 8192 | bytes 65536 | tf_op jit(solution)/shard_map/psum | solution.py:40
  114.3 0.0 copy-done.2
  114.3 0.1 fusion.11
  114.4 11.8 %psum.30 = f32[16]{0:T(128)S(1)} all-reduce(f32[16]{0:T(128)S(1)} %get-tuple-element.5), channel_id=1, replica_groups=mesh['section'=2,'tensor'=4,'dp'=4] {'section','dp'}, use_global_device_ids=true, to_apply=%region_7.8 | all-reduce | flops 16 | bytes 128 | tf_op jit(solution)/shard_map/psum | solution.py:16
  126.2 0.0 copy-done.3
  126.2 8.2 %fusion.17 = f32[16,2,7168]{2,0,1:T(8,128)} fusion(bf16[2,512,7168]{2,1,0:T(8,128)(2,1)} %param.20, bf16[16,512]{1,0:T(8,128)(2,1)S(1)} %get-tuple-element.6, f32[512]{0:T(512)S(1)} %copy-done.3, f32[16]{0:T(128)S(1)} %add_rsqrt_fusion), kind=kOutput, calls=%fused_computation.32 | convolution fusion | flops 234913792 | bytes 15616064 | tf_op jit(solution)/shard_map/rd,kdf->rkf/dot_general | solution.py:112
  134.4 0.0 all-reduce.7.cloned.1.call-update
  134.4 52.6 %all-reduce.7.cloned.1.call-done = f32[16,2,7168]{2,0,1:T(8,128)} async-done(((f32[16,2,7168]{2,0,1:T(8,128)}), f32[16,2,7168]{2,0,1:T(8,128)}) %all-reduce.7.cloned.1.call-update) | async-done | bytes 917520
  187.1 1.1 fusion.15
  188.2 8.6 %all-gather.1 = bf16[8,2,7168]{2,1,0:T(2,128)(2,1)S(1)} all-gather(bf16[1,2,7168]{2,1,0:T(2,128)(2,1)S(1)} %fusion.15), channel_id=1, replica_groups=mesh['section'=2,'tensor'=4,'dp'=4] {'section','dp'}, dimensions={0}, use_global_device_ids=true | all-gather | bytes 258048 | tf_op jit(solution)/shard_map/all_gather | solution.py:33
  196.8 0.1 reshape.132
  196.8 4.1 %fusion.38 = f32[16,512]{1,0:T(8,128)S(1)} fusion(bf16[16,7168]{1,0:T(8,128)(2,1)S(1)} %reshape.132, bf16[7168,512]{1,0:T(8,128)(2,1)} %param.21), kind=kOutput, calls=%fused_computation.66 | convolution fusion | flops 117440512 | bytes 7602176 | tf_op jit(solution)/shard_map/dot_general | solution.py:32
  201.0 19.0 %psum.31 = f32[16,512]{1,0:T(8,128)S(1)} all-reduce(f32[16,512]{1,0:T(8,128)S(1)} %fusion.38), channel_id=1, replica_groups=mesh['section'=2,'tensor'=4,'dp'=4] {'tensor'}, use_global_device_ids=true, to_apply=%region_9.10 | all-reduce | flops 8192 | bytes 65536 | tf_op jit(solution)/shard_map/psum | solution.py:40
  220.0 0.6 fusion.14
  (10 shorter events, 0.1 us)
Async XLA Ops:
  6.5 16.1 %copy-start = (bf16[512,2560]{1,0:T(8,128)(2,1)S(1)}, bf16[512,2560]{1,0:T(8,128)(2,1)}, u32[]{:S(2)}) copy-start(bf16[512,2560]{1,0:T(8,128)(2,1)} %param.13) | copy-start | bytes 7864324
  6.5 69.9 %all-reduce.5.cloned.1.call-start = ((), (), s32[]{:S(2)}) async-start(), calls=%async_computation | async-start | bytes 327680
  24.6 162.5 %all-reduce.7.cloned.1.call-start = ((), (), s32[]{:S(2)}) async-start(), calls=%async_computation.1 | async-start | bytes 1835008
  77.3 5.2 %copy-start.1 = (bf16[2,2,4096,128]{3,2,1,0:T(8,128)(2,1)S(1)}, bf16[2,2,4096,128]{3,2,1,0:T(8,128)(2,1)}, u32[]{:S(2)}) copy-start(bf16[2,2,4096,128]{3,2,1,0:T(8,128)(2,1)} %param.16) | copy-start | bytes 12582916
  82.2 32.0 %copy-start.2 = (bf16[16,512]{1,0:T(8,128)(2,1)S(1)}, bf16[16,512]{1,0:T(8,128)(2,1)}, u32[]{:S(2)}) copy-start(bf16[16,512]{1,0:T(8,128)(2,1)} %param.11) | copy-start | bytes 49156
  82.2 44.0 %copy-start.3 = (f32[512]{0:T(512)S(1)}, f32[512]{0:T(512)}, u32[]{:S(2)}) copy-start(f32[512]{0:T(512)} %param.19) | copy-start | bytes 6148
Sparse Core Ops, SparseCore 0:
  24.7 51.6 all-reduce.4
  134.6 52.4 all-reduce.6
where the time goes:
time: 228 us; the launch traced here: 227 us
  waiting for transfers between devices  101 us (44%)
  blocking collectives  83.5 us (37%)
  matrix products  21.5 us (9%)
  between operations  14.2 us (6%)
  other arithmetic  4.91 us (2%)
  local copies, waits for them, and re-layouts  2.31 us (1%)
    unnamed x4, waiting for transfers between devices  101 us
    psum x2, blocking collectives, add_residual(): summed = lax.psum(partial_sum, 'tensor')  38 us
    psum x2, blocking collectives, normalize(): squares = lax.psum(jnp.sum(wide * wide, axis=1), ('section', 'dp'))  27 us
    all_gather x2, blocking collectives, project_rows(): lax.all_gather(row_block, ('section', 'dp'), axis=0, tiled=True)  18.6 us
    dot_general x1, matrix products, body(): jnp.einsum('rd,kdf->rkf', row_block, gate_up, preferred_element_type=jnp....  8.21 us
    dot_general x2, matrix products, project_rows(): jnp.dot(lax.all_gather(row_block, ('section', 'dp'), axis=0, tiled=True),...  6.09 us
  transfers between devices with their start and end apart: 2, of which 2 were waited for; matrix products, arithmetic and copies ran while one was open for 1% of the time, Pallas kernels for 0%

commit v1 on v0

--- a/solution.py
+++ b/solution.py
@@ -9,6 +9,17 @@
 HD = 128
 LEN = 4096
 GROUP = 10
+
+
+def handle_sector(z_in):
+    mesh_ax = "tensor"
+    wide_n = lax.axis_size(mesh_ax)
+    parts_out = z_in
+    for num in [i for i in (1, 2, 4, 8, 16) if i < wide_n]:
+        parts_out = parts_out + lax.ppermute(
+            parts_out, mesh_ax, tuple(((h, h ^ num) for h in range(wide_n)))
+        )
+    return parts_out
 
 
 def normalize(stream, gain_vec):
@@ -37,7 +48,7 @@
 
 
 def add_residual(base_rows, partial_sum):
-    summed = lax.psum(partial_sum, "tensor")
+    summed = handle_sector(partial_sum)
     return (base_rows.astype(jnp.float32) + summed).astype(jnp.bfloat16)
 
 

time: 228 us -> 210 us (0.921)
  blocking collectives: 83.5 us -> 45.5 us
  waiting for transfers between devices: 101 us -> 114 us
  starting transfers between devices: 0.04 us -> 7.86 us
    psum x2 -> x0, blocking collectives: 38 us -> none  [add_residual(): summed = lax.psum(partial_sum, 'tensor')]
    ppermute x0 -> x4, waiting for transfers between devices: none -> 9.67 us  [handle_sector(): lax.ppermute(parts_out, mesh_ax, tuple(((h, h ^ num) for h in range(wide_...]
    ppermute x0 -> x4, starting transfers between devices: none -> 7.81 us  [handle_sector(): lax.ppermute(parts_out, mesh_ax, tuple(((h, h ^ num) for h in range(wide_...]
    unnamed x4, waiting for transfers between devices: 101 us -> 104 us
  transfers between devices with their start and end apart: 2 -> 6, of which waited for: 2 -> 6; matrix products, arithmetic and copies ran while one was open for 1% -> 1% of each run, Pallas kernels for 0% -> 0%
where the time goes in v1:
time: 210 us
  waiting for transfers between devices  114 us (54%)
  blocking collectives  45.5 us (22%)
  matrix products  21.5 us (10%)
  between operations  14.2 us (7%)
  starting transfers between devices  7.86 us (4%)
  other arithmetic  4.93 us (2%)
  local copies, waits for them, and re-layouts  2.31 us (1%)
    unnamed x4, waiting for transfers between devices  104 us
    psum x2, blocking collectives, normalize(): squares = lax.psum(jnp.sum(wide * wide, axis=1), ('section', 'dp'))  27 us
    all_gather x2, blocking collectives, project_rows(): lax.all_gather(row_block, ('section', 'dp'), axis=0, tiled=True)  18.6 us
    ppermute x4, waiting for transfers between devices, handle_sector(): lax.ppermute(parts_out, mesh_ax, tuple(((h, h ^ num) for h in range(wide_...  9.67 us
    dot_general x1, matrix products, body(): jnp.einsum('rd,kdf->rkf', row_block, gate_up, preferred_element_type=jnp....  8.21 us
    ppermute x4, starting transfers between devices, handle_sector(): lax.ppermute(parts_out, mesh_ax, tuple(((h, h ^ num) for h in range(wide_...  7.81 us
    dot_general x2, matrix products, project_rows(): jnp.dot(lax.all_gather(row_block, ('section', 'dp'), axis=0, tiled=True),...  6.09 us
  transfers between devices with their start and end apart: 6, of which 6 were waited for; matrix products, arithmetic and copies ran while one was open for 1% of the time, Pallas kernels for 0%

profile of v1, /device:TPU:0, one launch (start us, length us, event | category | flops | bytes accessed | tf_op | source)
XLA Modules:
  0.0 210.0 jit_solution(15147693219271510701)
XLA Ops:
  6.5 0.0 copy-start
  6.5 0.0 all-reduce.5.cloned.1.call-start
  6.5 1.0 fusion.7
  7.5 15.1 %psum.14 = f32[16]{0:T(128)S(1)} all-reduce(f32[16]{0:T(128)S(1)} %fusion.7), channel_id=1, replica_groups=mesh['section'=2,'tensor'=4,'dp'=4] {'section','dp'}, use_global_device_ids=true, to_apply=%region_1.0 | all-reduce | flops 16 | bytes 128 | tf_op jit(solution)/shard_map/psum | solution.py:27
  22.7 0.0 copy-done
  22.7 1.9 fusion.19
  24.6 0.0 all-reduce.5.cloned.1.call-update
  24.6 0.0 all-reduce.7.cloned.1.call-start
  24.6 0.7 convert_element_type.47
  25.3 0.7 iota_compare_fusion
  26.0 0.1 multiply_cosine_fusion
  26.2 1.2 dynamic-slice
  28.1 48.3 %all-reduce.5.cloned.1.call-done = f32[16,2560]{1,0:T(8,128)} async-done(((f32[16,2560]{1,0:T(8,128)}), f32[16,2560]{1,0:T(8,128)}) %all-reduce.5.cloned.1.call-update) | async-done | bytes 163856
  76.4 0.9 constant_dynamic-slice_fusion
  77.3 0.0 copy-start.1
  77.3 0.9 convolution_bitcast_fusion
  78.3 0.1 subtract_convert_fusion
  78.4 0.1 subtract_convert_fusion.1
  78.5 0.1 maximum_bitcast_fusion
  78.5 0.2 fusion.29
  78.7 3.5 %fusion.36 = (f32[2,2,8]{2,1,0:T(2,128)S(1)}, f32[2,2,8,4096]{3,2,1,0:T(8,128)S(1)}) fusion(bf16[2,2,4096,128]{3,2,1,0:T(8,128)(2,1)} %param.15, bf16[2,2,8,64]{3,2,1,0:T(8,128)(2,1)S(1)} %get-tuple-element.8, bf16[2,2,8,64]{3,2,1,0:T(8,128)(2,1)S(1)} %get-tuple-element.7, pred[2,4096]{1,0:T(4,128)(4,1)S(1)} %iota_compare_fusion), kind=kOutput, calls=%fused_computation.64 | convolution fusion | flops 33964000 | bytes 4735104 | tf_op jit(solution)/shard_map/bgpd,bgld->bgpl/dot_general | solution.py:96
  82.2 0.0 copy-start.2
  82.2 0.0 copy-start.3
  82.3 0.2 fusion.2
  82.5 0.0 copy-done.1
  82.5 0.7 fusion.1
  83.3 10.0 %all-gather = bf16[8,2,2048]{2,1,0:T(2,128)(2,1)S(1)} all-gather(bf16[1,2,2048]{2,1,0:T(2,128)(2,1)S(1)} %reshape.129), channel_id=1, replica_groups=mesh['section'=2,'tensor'=4,'dp'=4] {'section','dp'}, dimensions={0}, use_global_device_ids=true | all-gather | bytes 73728 | tf_op jit(solution)/shard_map/all_gather | solution.py:44
  93.3 2.0 fusion.37
  95.3 1.5 collective-permute-start
  96.8 2.4 %collective-permute-done = f32[16,512]{1,0:T(8,128)S(1)} collective-permute-done((f32[16,512]{1,0:T(8,128)S(1)}, f32[16,512]{1,0:T(8,128)S(1)}, u32[]{:S(2)}, u32[]{:S(2)}) %collective-permute-start) | collective-permute-done | bytes 32800 | tf_op jit(solution)/shard_map/ppermute | solution.py:19
  99.2 2.4 %collective-permute-start.1 = (f32[16,512]{1,0:T(8,128)S(1)}, f32[16,512]{1,0:T(8,128)S(1)}, u32[]{:S(2)}, u32[]{:S(2)}) collective-permute-start(f32[16,512]{1,0:T(8,128)S(1)} %add.53), channel_id=1, source_target_pairs={{0,8},{4,12},{8,0},{12,4},{1,9},{5,13},{9,1},{13,5},{2,10},{6,14},... | collective-permute-start | bytes 98312 | tf_op jit(solution)/shard_map/ppermute | solution.py:19
  101.6 2.4 %collective-permute-done.1 = f32[16,512]{1,0:T(8,128)S(1)} collective-permute-done((f32[16,512]{1,0:T(8,128)S(1)}, f32[16,512]{1,0:T(8,128)S(1)}, u32[]{:S(2)}, u32[]{:S(2)}) %collective-permute-start.1) | collective-permute-done | bytes 32800 | tf_op jit(solution)/shard_map/ppermute | solution.py:19
  104.0 0.0 copy-done.2
  104.0 0.1 fusion.11
  104.1 11.8 %psum.15 = f32[16]{0:T(128)S(1)} all-reduce(f32[16]{0:T(128)S(1)} %get-tuple-element.5), channel_id=1, replica_groups=mesh['section'=2,'tensor'=4,'dp'=4] {'section','dp'}, use_global_device_ids=true, to_apply=%region_6.7 | all-reduce | flops 16 | bytes 128 | tf_op jit(solution)/shard_map/psum | solution.py:27
  116.0 0.0 copy-done.3
  116.0 8.2 %fusion.17 = f32[16,2,7168]{2,0,1:T(8,128)} fusion(bf16[2,512,7168]{2,1,0:T(8,128)(2,1)} %param.20, bf16[16,512]{1,0:T(8,128)(2,1)S(1)} %get-tuple-element.6, f32[512]{0:T(512)S(1)} %copy-done.3, f32[16]{0:T(128)S(1)} %add_rsqrt_fusion), kind=kOutput, calls=%fused_computation.32 | convolution fusion | flops 234913792 | bytes 15616064 | tf_op jit(solution)/shard_map/rd,kdf->rkf/dot_general | solution.py:123
  124.2 0.0 all-reduce.7.cloned.1.call-update
  124.2 55.7 %all-reduce.7.cloned.1.call-done = f32[16,2,7168]{2,0,1:T(8,128)} async-done(((f32[16,2,7168]{2,0,1:T(8,128)}), f32[16,2,7168]{2,0,1:T(8,128)}) %all-reduce.7.cloned.1.call-update) | async-done | bytes 917520
  179.9 1.1 fusion.15
  181.0 8.6 %all-gather.1 = bf16[8,2,7168]{2,1,0:T(2,128)(2,1)S(1)} all-gather(bf16[1,2,7168]{2,1,0:T(2,128)(2,1)S(1)} %fusion.15), channel_id=1, replica_groups=mesh['section'=2,'tensor'=4,'dp'=4] {'section','dp'}, dimensions={0}, use_global_device_ids=true | all-gather | bytes 258048 | tf_op jit(solution)/shard_map/all_gather | solution.py:44
  189.6 0.1 reshape.132
  189.7 4.1 %fusion.38 = f32[16,512]{1,0:T(8,128)S(1)} fusion(bf16[16,7168]{1,0:T(8,128)(2,1)S(1)} %reshape.132, bf16[7168,512]{1,0:T(8,128)(2,1)} %param.21), kind=kOutput, calls=%fused_computation.66 | convolution fusion | flops 117440512 | bytes 7602176 | tf_op jit(solution)/shard_map/dot_general | solution.py:43
  193.8 1.5 collective-permute-start.2
  195.3 2.4 %collective-permute-done.2 = f32[16,512]{1,0:T(8,128)S(1)} collective-permute-done((f32[16,512]{1,0:T(8,128)S(1)}, f32[16,512]{1,0:T(8,128)S(1)}, u32[]{:S(2)}, u32[]{:S(2)}) %collective-permute-start.2) | collective-permute-done | bytes 32800 | tf_op jit(solution)/shard_map/ppermute | solution.py:19
  197.7 2.4 %collective-permute-start.3 = (f32[16,512]{1,0:T(8,128)S(1)}, f32[16,512]{1,0:T(8,128)S(1)}, u32[]{:S(2)}, u32[]{:S(2)}) collective-permute-start(f32[16,512]{1,0:T(8,128)S(1)} %add.58), channel_id=1, source_target_pairs={{0,8},{4,12},{8,0},{12,4},{1,9},{5,13},{9,1},{13,5},{2,10},{6,14},... | collective-permute-start | bytes 98312 | tf_op jit(solution)/shard_map/ppermute | solution.py:19
  200.1 2.4 %collective-permute-done.3 = f32[16,512]{1,0:T(8,128)S(1)} collective-permute-done((f32[16,512]{1,0:T(8,128)S(1)}, f32[16,512]{1,0:T(8,128)S(1)}, u32[]{:S(2)}, u32[]{:S(2)}) %collective-permute-start.3) | collective-permute-done | bytes 32800 | tf_op jit(solution)/shard_map/ppermute | solution.py:19
  202.5 0.6 fusion.14
  (12 shorter events, 0.1 us)
Async XLA Ops:
  6.5 16.1 %copy-start = (bf16[512,2560]{1,0:T(8,128)(2,1)S(1)}, bf16[512,2560]{1,0:T(8,128)(2,1)}, u32[]{:S(2)}) copy-start(bf16[512,2560]{1,0:T(8,128)(2,1)} %param.13) | copy-start | bytes 7864324
  6.5 69.9 %all-reduce.5.cloned.1.call-start = ((), (), s32[]{:S(2)}) async-start(), calls=%async_computation | async-start | bytes 327680
  24.6 155.3 %all-reduce.7.cloned.1.call-start = ((), (), s32[]{:S(2)}) async-start(), calls=%async_computation.1 | async-start | bytes 1835008
  77.3 5.2 %copy-start.1 = (bf16[2,2,4096,128]{3,2,1,0:T(8,128)(2,1)S(1)}, bf16[2,2,4096,128]{3,2,1,0:T(8,128)(2,1)}, u32[]{:S(2)}) copy-start(bf16[2,2,4096,128]{3,2,1,0:T(8,128)(2,1)} %param.16) | copy-start | bytes 12582916
  82.2 21.8 %copy-start.2 = (bf16[16,512]{1,0:T(8,128)(2,1)S(1)}, bf16[16,512]{1,0:T(8,128)(2,1)}, u32[]{:S(2)}) copy-start(bf16[16,512]{1,0:T(8,128)(2,1)} %param.11) | copy-start | bytes 49156
  82.2 33.7 %copy-start.3 = (f32[512]{0:T(512)S(1)}, f32[512]{0:T(512)}, u32[]{:S(2)}) copy-start(f32[512]{0:T(512)} %param.19) | copy-start | bytes 6148
  95.3 3.9 %collective-permute-start = (f32[16,512]{1,0:T(8,128)S(1)}, f32[16,512]{1,0:T(8,128)S(1)}, u32[]{:S(2)}, u32[]{:S(2)}) collective-permute-start(f32[16,512]{1,0:T(8,128)S(1)} %fusion.37), channel_id=1, source_target_pairs={{0,4},{4,0},{8,12},{12,8},{1,5},{5,1},{9,13},{13,9},{2,6},{6,2},{1... | collective-permute-start | bytes 98312 | tf_op jit(solution)/shard_map/ppermute | solution.py:19
  99.2 4.8 %collective-permute-start.1 = (f32[16,512]{1,0:T(8,128)S(1)}, f32[16,512]{1,0:T(8,128)S(1)}, u32[]{:S(2)}, u32[]{:S(2)}) collective-permute-start(f32[16,512]{1,0:T(8,128)S(1)} %add.53), channel_id=1, source_target_pairs={{0,8},{4,12},{8,0},{12,4},{1,9},{5,13},{9,1},{13,5},{2,10},{6,14},... | collective-permute-start | bytes 98312 | tf_op jit(solution)/shard_map/ppermute | solution.py:19
  193.8 3.9 %collective-permute-start.2 = (f32[16,512]{1,0:T(8,128)S(1)}, f32[16,512]{1,0:T(8,128)S(1)}, u32[]{:S(2)}, u32[]{:S(2)}) collective-permute-start(f32[16,512]{1,0:T(8,128)S(1)} %fusion.38), channel_id=1, source_target_pairs={{0,4},{4,0},{8,12},{12,8},{1,5},{5,1},{9,13},{13,9},{2,6},{6,2},{1... | collective-permute-start | bytes 98312 | tf_op jit(solution)/shard_map/ppermute | solution.py:19
  197.7 4.8 %collective-permute-start.3 = (f32[16,512]{1,0:T(8,128)S(1)}, f32[16,512]{1,0:T(8,128)S(1)}, u32[]{:S(2)}, u32[]{:S(2)}) collective-permute-start(f32[16,512]{1,0:T(8,128)S(1)} %add.58), channel_id=1, source_target_pairs={{0,8},{4,12},{8,0},{12,4},{1,9},{5,13},{9,1},{13,5},{2,10},{6,14},... | collective-permute-start | bytes 98312 | tf_op jit(solution)/shard_map/ppermute | solution.py:19
Sparse Core Ops, SparseCore 0:
  24.7 51.6 all-reduce.4
  124.3 55.5 all-reduce.6
